TPU v7x, 16 devices: a whole 2x2x2 slice. The times are simulated.
16 devices in a mesh: dp: 1, ep: 16 (over x, y, z, core).
Axes of the slice: x: 2, y: 2, z: 2, core: 2. Of those that a mesh axis runs over, the one named last changes fastest.
Arguments:
- x: bfloat16 [1, 16, 256, 4096], P('dp', 'ep')
- expert: int32 [1, 16, 256, 8], P('dp', 'ep')
- slot: int32 [1, 16, 256, 8], P('dp', 'ep')
- gate: float32 [1, 16, 256, 8], P('dp', 'ep')
- w_gate: bfloat16 [64, 4096, 1536], P('ep')
- w_up: bfloat16 [64, 4096, 1536], P('ep')
- w_down: bfloat16 [64, 1536, 4096], P('ep')
Outputs:
- y: bfloat16 [1, 16, 256, 4096], P('dp', 'ep')
All inputs are finite; a program needn't handle non-finite values.
Results may differ from a plain program's by a relative error of at most 0.009.
Values are sent between devices in bfloat16 or wider.
A program may use at most 2 GiB of HBM per device.

v0:
```python
import jax
import jax.numpy as jnp
from jax import lax
from jax.sharding import NamedSharding, PartitionSpec as P


def einsum(form, a, b):
    return jnp.einsum(form, a.astype(jnp.float32), b.astype(jnp.float32))


def solution(mesh):
    def placed(v, *spec):
        return lax.with_sharding_constraint(v, NamedSharding(mesh, P(*spec)))

    def step(x, expert, slot, gate, w_gate, w_up, w_down):
        experts, (tokens, top) = w_gate.shape[0], expert.shape[2:]
        slots = 5 * tokens * top // (4 * experts)
        to_expert = jax.nn.one_hot(expert, experts, dtype=jnp.bfloat16)
        to_slot = jax.nn.one_hot(slot, slots, dtype=jnp.bfloat16)
        weighted = to_expert * gate[..., None].astype(jnp.bfloat16)
        dispatch = einsum("abtke,abtkc->abtec", to_expert, to_slot).astype(jnp.bfloat16)
        combine = einsum("abtke,abtkc->abtec", weighted, to_slot).astype(jnp.bfloat16)
        z = einsum("abtec,abtd->aebcd", dispatch, x).astype(jnp.bfloat16)
        z = placed(z, "dp", None, "ep", None, None)
        z = placed(z, "dp", "ep", None, None, None)
        h = jax.nn.silu(einsum("aebcd,edf->aebcf", z, w_gate))
        h = (h * einsum("aebcd,edf->aebcf", z, w_up)).astype(jnp.bfloat16)
        out = einsum("aebcf,efd->aebcd", h, w_down).astype(jnp.bfloat16)
        out = placed(out, "dp", "ep", None, None, None)
        out = placed(out, "dp", None, "ep", None, None)
        y = einsum("abtec,aebcd->abtd", combine, out)
        return y.astype(jnp.bfloat16)

    return step
```

profile of v0, /device:TPU:0, one launch (start us, length us, event | category | flops | bytes accessed | tf_op | source)
XLA Modules:
  0.0 772.4 jit_solution(5541695726985636125)
XLA Ops:
  0.0 0.0 copy-start
  0.0 1.0 copy.10
  1.0 0.0 copy-start.2
  1.0 0.8 copy.12
  1.8 0.0 copy-done.2
  1.8 0.0 copy-start.4
  1.9 0.6 copy-done.4
  2.5 3.6 convolution_convert_fusion.1
  6.1 5.6 copy.13
  11.7 0.0 copy-done
  11.8 10.2 %convolution_convert_fusion = bf16[64,40,4096]{2,1,0:T(8,128)(2,1)} fusion(bf16[256,64,40]{0,2,1:T(8,128)(2,1)S(1)} %copy.13, bf16[1,1,256,4096]{3,2,1,0:T(8,128)(2,1)S(1)} %copy-done), kind=kOutput, calls=%fused_computation.18 | convolution fusion | flops 5379194880 | bytes 24379392 | tf_op jit(solution)/abtec,abtd->aebcd/dot_general | solution.py:8
  21.9 235.5 %all-to-all.4 = bf16[1,16,4,1,40,4096]{5,4,2,3,0,1:T(8,128)(2,1)} all-to-all(bf16[1,16,4,1,40,4096]{5,4,2,3,0,1:T(8,128)(2,1)} %bitcast.120), channel_id=1, replica_groups=mesh['dp'=1,'ep'=16] {'ep'}, dimensions={1} | all-to-all | bytes 41943040 | tf_op jit(solution)/sharding_constraint;jit(solution)/sharding_constraint | solution.py:13
  257.5 41.2 %fusion.2 = f32[4,16,40,1536]{3,2,1,0:T(8,128)} fusion(bf16[4,4096,1536]{2,1,0:T(8,128)(2,1)} %param.5, bf16[1,16,4,1,40,4096]{5,4,2,3,0,1:T(8,128)(2,1)} %all-to-all.4), kind=kOutput, calls=%fused_computation.2 | convolution fusion | flops 32212254720 | bytes 87031808 | tf_op jit(solution)/aebcd,edf->aebcf/dot_general | solution.py:8
  298.7 41.3 %fusion.4 = f32[4,16,40,1536]{3,2,1,0:T(8,128)} fusion(bf16[4,4096,1536]{2,1,0:T(8,128)(2,1)} %param.4, bf16[1,16,4,1,40,4096]{5,4,2,3,0,1:T(8,128)(2,1)} %all-to-all.4), kind=kOutput, calls=%fused_computation.4 | convolution fusion | flops 32212254720 | bytes 87031808 | tf_op jit(solution)/aebcd,edf->aebcf/dot_general | solution.py:8
  340.0 49.4 %convert_bitcast_fusion = bf16[1,4,16,1,40,4096]{5,4,2,1,3,0:T(8,128)(2,1)} fusion(bf16[4,1536,4096]{2,1,0:T(8,128)(2,1)} %param.6, f32[4,16,40,1536]{3,2,1,0:T(8,128)} %fusion.2, f32[4,16,40,1536]{3,2,1,0:T(8,128)} %fusion.4), kind=kOutput, calls=%fused_computation.8 | convolution fusion | flops 32246333440 | bytes 102760448 | tf_op jit(solution)/aebcf,efd->aebcd/dot_general | solution.py:8
  389.3 17.5 %copy.16 = bf16[1,4,16,1,40,4096]{5,4,1,3,0,2:T(8,128)(2,1)} copy(bf16[1,4,16,1,40,4096]{5,4,2,1,3,0:T(8,128)(2,1)} %convert_bitcast_fusion) | data formatting | bytes 41943040 | tf_op jit(solution)/sharding_constraint;jit(solution)/sharding_constraint | solution.py:13
  406.8 0.0 copy-start.6
  406.8 0.0 copy-start.3
  406.8 0.0 copy-start.5
  406.8 4.2 all-to-all-start.1
  411.1 0.0 copy-done.6
  411.1 0.1 copy.11
  411.2 0.0 copy-done.3
  411.2 0.0 copy-done.5
  411.2 0.0 copy-start.1
  411.3 4.3 convolution_convert_fusion.2
  415.5 5.6 copy.23
  421.2 339.8 %all-to-all-done.1 = bf16[1,4,16,1,40,4096]{5,4,1,3,0,2:T(8,128)(2,1)} async-done(((bf16[1,4,16,1,40,4096]{5,4,1,3,0,2:T(8,128)(2,1)}), bf16[1,4,16,1,40,4096]{5,4,1,3,0,2:T(8,128)(2,1)}, u32[]{:S(2)}, u32[]{:S(2)}) %all-to-all-start.1) | async-done | bytes 20971552 | tf_op jit(solution)/sharding_constraint;jit(solution)/sharding_constraint | solution.py:13
  761.0 11.5 %fusion.19 = bf16[1,1,256,4096]{3,2,1,0:T(8,128)(2,1)} fusion(bf16[256,64,40]{0,2,1:T(8,128)(2,1)S(1)} %copy.23, bf16[64,40,4096]{2,1,0:T(8,128)(2,1)} %bitcast.38), kind=kOutput, calls=%fused_computation.22 | convolution fusion | flops 5369757696 | bytes 24379392 | tf_op jit(solution)/abtec,aebcd->abtd/dot_general | solution.py:8
  772.4 0.0 copy-done.1
  (1 shorter events, 0.0 us)
Async XLA Ops:
  0.0 11.7 %copy-start = (bf16[1,1,256,4096]{3,2,1,0:T(8,128)(2,1)S(1)}, bf16[1,1,256,4096]{3,2,1,0:T(8,128)(2,1)}, u32[]{:S(2)}) copy-start(bf16[1,1,256,4096]{3,2,1,0:T(8,128)(2,1)} %param.3) | copy-start | bytes 6291460
  1.0 0.9 copy-start.2
  1.8 0.7 copy-start.4
  406.8 4.3 copy-start.6
  406.8 4.4 copy-start.3
  406.8 4.4 copy-start.5
  406.8 354.1 %all-to-all-start.1 = ((bf16[1,4,16,1,40,4096]{5,4,1,3,0,2:T(8,128)(2,1)}), bf16[1,4,16,1,40,4096]{5,4,1,3,0,2:T(8,128)(2,1)}, u32[]{:S(2)}, u32[]{:S(2)}) async-start(bf16[1,4,16,1,40,4096]{5,4,1,3,0,2:T(8,128)(2,1)} %copy.16), calls=%async_computation.1 | async-start | bytes 41943040 | tf_op jit(solution)/sharding_constraint;jit(solution)/sharding_constraint | solution.py:13
  411.2 361.2 %copy-start.1 = (bf16[1,1,256,4096]{3,2,1,0:T(8,128)(2,1)S(1)}, bf16[1,1,256,4096]{3,2,1,0:T(8,128)(2,1)}, u32[]{:S(2)}) copy-start(bf16[1,1,256,4096]{3,2,1,0:T(8,128)(2,1)} %param.3) | copy-start | bytes 6291460
where the time goes:
time: 773 us; the launch traced here: 772 us
  waiting for transfers between devices  340 us (44%)
  blocking collectives  236 us (31%)
  matrix products  161 us (21%)
  local copies, waits for them, and re-layouts  31.3 us (4%)
    another operation x1, waiting for transfers between devices, placed(): return lax.with_sharding_constraint(v, NamedSharding(mesh, P(*spec)))  340 us
    another operation x1, blocking collectives, placed(): return lax.with_sharding_constraint(v, NamedSharding(mesh, P(*spec)))  236 us
    dot_general x7, matrix products, einsum(): return jnp.einsum(form, a.astype(jnp.float32), b.astype(jnp.float32))  161 us
    another operation x1, local copies, waits for them, and re-layouts, placed(): return lax.with_sharding_constraint(v, NamedSharding(mesh, P(*spec)))  17.5 us
  transfers between devices with their start and end apart: 1, of which 1 were waited for; matrix products, arithmetic and copies ran while one was open for 1% of the time, Pallas kernels for 0%

commit v1 on v0

v1 whole, which is shorter than its diff:
```python
import functools

import jax
import jax.numpy as jnp
import numpy as np
from jax import lax
from jax.experimental import pallas as pl
from jax.experimental.pallas import tpu as pltpu
from jax.sharding import PartitionSpec as P

MESH = pl.DeviceIdType.MESH
CHIPS = 8
WEIGHT = (8, 4, 2)
ROWS = ((0, 88), (88, 88), (176, 80))
KC = 512


def bit(me, d):
    return lax.rem(me // WEIGHT[d], 2)


def flip(me, d):
    return me + WEIGHT[d] * (1 - 2 * bit(me, d))


def gather_kernel(
    slots, x_ref, meta_ref, rid_ref, wg_ref, wu_ref,
    xg_ref, c_ref, h_ref,
    allm, dmat, cbuf, own, xb, z, wg, wu, acc_g, acc_u, hb,
    s1, s2, s3, d2d, send, meta_send, meta_recv, own_sem, c_sem, x_sem, w_sem, h_sem,
):
    me = lax.axis_index("ep")
    core = lax.rem(me, 2)
    chip = me // 2
    partner = me + 1 - 2 * core
    tokens, depth = x_ref.shape
    chunks = depth // KC
    experts, _, ff = wg_ref.shape
    pair = 2 * slots
    rows = experts * pair

    def cols(j):
        return pl.ds(pl.multiple_of(j * KC, KC), KC)

    def part(idx, r, j):
        return xg_ref.at[idx // 2, lax.rem(idx, 2), pl.ds(*ROWS[r]), cols(j)]

    def own_part(r, j):
        return x_ref.at[pl.ds(*ROWS[r]), cols(j)]

    def push(src, idx, r, j, sem, to):
        pltpu.make_async_remote_copy(
            src_ref=src, dst_ref=part(idx, r, j), send_sem=send, recv_sem=sem.at[j, r],
            device_id={"ep": to}, device_id_type=MESH,
        ).start()

    def await_parts(n, r, j, sem):
        ref = xg_ref.at[pl.ds(0, n), 0, pl.ds(*ROWS[r]), cols(j)]
        pltpu.make_async_copy(ref, ref, sem.at[j, r]).wait()

    def stage_a(j):
        for r in range(3):
            push(own_part(r, j), me, r, j, s1, flip(me, r))
        for r in range(3):
            push(own_part(r, j), me, r, j, s2, flip(me, (r + 1) % 3))
        for r in range(3):
            push(own_part(r, j), me, r, j, s3, flip(me, (r + 2) % 3))

    def stage_b(j):
        for r in range(3):
            await_parts(1, r, j, s1)
            a = flip(me, r)
            push(part(a, r, j), a, r, j, s2, flip(me, (r + 1) % 3))
            push(part(a, r, j), a, r, j, s3, flip(me, (r + 2) % 3))

    def stage_c(j):
        for r in range(3):
            await_parts(2, r, j, s2)
            b = flip(me, (r + 1) % 3)
            ab = flip(b, r)
            push(part(b, r, j), b, r, j, s3, flip(me, (r + 2) % 3))
            push(part(ab, r, j), ab, r, j, s3, flip(me, (r + 2) % 3))

    def stage_e(j):
        for r in range(3):
            await_parts(4, r, j, s3)
        ref = xg_ref.at[:, core, :, cols(j)]
        pltpu.make_async_remote_copy(
            src_ref=ref, dst_ref=ref, send_sem=send, recv_sem=d2d.at[j],
            device_id={"ep": partner}, device_id_type=MESH,
        ).start()

    def await_d2d(j):
        ref = xg_ref.at[:, 0, :, cols(j)]
        pltpu.make_async_copy(ref, ref, d2d.at[j]).wait()

    def load_x(j):
        k = lax.rem(j, 2)
        return pltpu.make_async_copy(xg_ref.at[:, :, :, cols(j)], xb.at[k], x_sem.at[k])

    def load_w(q):
        j, e, k = q // experts, lax.rem(q, experts), lax.rem(q, 2)
        src = pl.ds(pl.multiple_of(j * KC, KC), KC)
        return (
            pltpu.make_async_copy(wg_ref.at[e, src, :], wg.at[k], w_sem.at[0, k]),
            pltpu.make_async_copy(wu_ref.at[e, src, :], wu.at[k], w_sem.at[1, k]),
        )

    def own_copy(i):
        half = tokens // 2
        at = pl.ds(i * half, half)
        a = pltpu.make_async_copy(x_ref.at[at, :], own, own_sem)
        a.start()
        a.wait()
        b = pltpu.make_async_copy(own, xg_ref.at[chip, core, at, :], own_sem)
        b.start()
        b.wait()

    barrier = pltpu.get_barrier_semaphore()
    for d in range(1, 16):
        pl.semaphore_signal(barrier, inc=1, device_id={"ep": lax.rem(me + d, 16)}, device_id_type=MESH)
    pl.semaphore_wait(barrier, 15)

    stage_a(0)
    for d in range(1, 16):
        pltpu.make_async_remote_copy(
            src_ref=meta_ref, dst_ref=allm.at[me], send_sem=meta_send, recv_sem=meta_recv,
            device_id={"ep": lax.rem(me + d, 16)}, device_id_type=MESH,
        ).start()
    stage_a(1)
    for w in load_w(0):
        w.start()
    mine = pltpu.make_async_copy(meta_ref, allm.at[me], own_sem)
    mine.start()
    mine.wait()
    own_copy(0)
    own_copy(1)
    stage_b(0)

    acc_g[...] = jnp.zeros_like(acc_g)
    acc_u[...] = jnp.zeros_like(acc_u)
    others = allm.at[pl.ds(0, 15)]
    pltpu.make_async_copy(others, others, meta_recv).wait()
    pltpu.make_async_copy(others, others, meta_send).wait()
    stage_a(2)
    stage_b(1)
    stage_c(0)

    base = (me * (experts * slots)).astype(jnp.float32)
    for s2_ in range(2):
        rid = rid_ref[s2_]
        rid = jnp.concatenate([rid, rid], axis=1)
        rid = jnp.where(rid < 0, rid, rid + base)

        @pl.loop(0, CHIPS)
        def _(p):
            m = allm[2 * p + s2_]
            d = jnp.zeros((rows, tokens), jnp.float32)
            c = jnp.zeros((rows, tokens), jnp.float32)
            for k in range(8):
                hit = rid == m[k:k + 1, :]
                d = jnp.where(hit, 1.0, d)
                c = jnp.where(hit, m[8 + k:9 + k, :], c)
            dmat[p, :, s2_ * tokens:(s2_ + 1) * tokens] = d.astype(jnp.bfloat16)
            cbuf[p, s2_] = c.T.astype(jnp.bfloat16)

    put_c = pltpu.make_async_copy(cbuf, c_ref, c_sem)
    put_c.start()

    def step(i, _):
        live = i >= 1
        j = jnp.maximum(i - 1, 0)
        k = lax.rem(j, 2)

        @pl.when(live)
        def _():
            load_x(j).wait()

            @pl.loop(0, CHIPS)
            def _(p):
                tok = xb[k, p].reshape(2 * tokens, KC)
                got = jnp.dot(dmat[p], tok, preferred_element_type=jnp.float32).astype(jnp.bfloat16)
                at = pl.ds(pl.multiple_of(p * pair, 16), pair)
                for e in range(experts):
                    z[e, at, :] = got[e * pair:(e + 1) * pair]

        def expert(e):
            @pl.when(live)
            def _():
                q = j * experts + e
                kw = lax.rem(q, 2)
                for w in load_w(q):
                    w.wait()

                @pl.when(q + 1 < chunks * experts)
                def _():
                    for w in load_w(q + 1):
                        w.start()

                @pl.loop(0, ff // 512)
                def _(n):
                    at = pl.ds(pl.multiple_of(n * 512, 512), 512)
                    acc_g[e, :, at] += jnp.dot(z[e], wg[kw, :, at], preferred_element_type=jnp.float32)
                    acc_u[e, :, at] += jnp.dot(z[e], wu[kw, :, at], preferred_element_type=jnp.float32)

        expert(0)

        @pl.when(i + 3 < chunks)
        def _():
            stage_a(i + 3)

        @pl.when(i + 2 < chunks)
        def _():
            stage_b(i + 2)

        expert(1)

        @pl.when(i < chunks)
        def _():
            stage_e(i)

        expert(2)

        @pl.when(i + 1 < chunks)
        def _():
            stage_c(i + 1)

        expert(3)

        @pl.when(i < chunks)
        def _():
            await_d2d(i)
            load_x(i).start()

        return 0

    lax.fori_loop(0, chunks + 1, step, 0)

    for e in range(experts):
        put = pltpu.make_async_copy(hb.at[e % 2], h_ref.at[e], h_sem.at[e % 2])
        if e >= 2:
            put.wait()

        @pl.loop(0, 8)
        def _(b):
            at = pl.ds(pl.multiple_of(b * pair, 16), pair)
            g = acc_g[e, at, :]
            hb[e % 2, at, :] = (g / (1.0 + jnp.exp(-g)) * acc_u[e, at, :]).astype(jnp.bfloat16)

        put.start()
    put_c.wait()
    for e in range(experts - 2, experts):
        pltpu.make_async_copy(hb.at[e % 2], h_ref.at[e], h_sem.at[e % 2]).wait()
    sent = xg_ref.at[:, :, :, pl.ds(0, depth - depth // 16)]
    pltpu.make_async_copy(sent, sent, send).wait()


ANY = pl.BlockSpec(memory_space=pl.ANY)
VM = pl.BlockSpec(memory_space=pltpu.VMEM)


def gather_call(slots, x, meta, rid, wg, wu):
    tokens, depth = x.shape
    experts, _, ff = wg.shape
    chunks = depth // KC
    rows = experts * 2 * slots
    per = 16 * slots
    bf, f32 = jnp.bfloat16, jnp.float32
    dma = pltpu.SemaphoreType.DMA
    return pl.pallas_call(
        functools.partial(gather_kernel, slots),
        out_shape=(
            jax.ShapeDtypeStruct((CHIPS, 2, tokens, depth), bf),
            jax.ShapeDtypeStruct((CHIPS, 2, tokens, rows), bf),
            jax.ShapeDtypeStruct((experts, per, ff), bf),
        ),
        in_specs=[ANY, VM, VM, ANY, ANY],
        out_specs=(ANY, ANY, ANY),
        scratch_shapes=[
            pltpu.VMEM((16, 16, tokens), f32),
            pltpu.VMEM((CHIPS, rows, 2 * tokens), bf),
            pltpu.VMEM((CHIPS, 2, tokens, rows), bf),
            pltpu.VMEM((tokens // 2, depth), bf),
            pltpu.VMEM((2, CHIPS, 2, tokens, KC), bf),
            pltpu.VMEM((experts, per, KC), bf),
            pltpu.VMEM((2, KC, ff), bf),
            pltpu.VMEM((2, KC, ff), bf),
            pltpu.VMEM((experts, per, ff), f32),
            pltpu.VMEM((experts, per, ff), f32),
            pltpu.VMEM((2, per, ff), bf),
            dma((chunks, 3)), dma((chunks, 3)), dma((chunks, 3)), dma((chunks,)),
            dma, dma, dma, dma, dma, dma((2,)), dma((2, 2)), dma((2,)),
        ],
        compiler_params=pltpu.CompilerParams(
            collective_id=0, has_side_effects=True, vmem_limit_bytes=67_000_000
        ),
        name="gather_up",
    )(x, meta, rid, wg, wu)


def np_rid(experts, slots):
    e, s, c = np.meshgrid(np.arange(experts), np.arange(2), np.arange(slots), indexing="ij")
    rid = np.where(s.reshape(1, -1) == np.arange(2)[:, None], (e * slots + c).reshape(1, -1), -7)
    return jnp.broadcast_to(jnp.asarray(rid, jnp.float32)[:, :, None], (*rid.shape, 128))


def solution(mesh):
    def step(x, expert, slot, gate, w_gate, w_up, w_down):
        x, expert, slot, gate = x[0, 0], expert[0, 0], slot[0, 0], gate[0, 0]
        tokens, top = expert.shape
        total = 16 * w_gate.shape[0]
        slots = 5 * tokens * top // (4 * total)
        number = jnp.where(slot < slots, expert * slots + slot, -1).astype(jnp.float32)
        weight = gate.astype(jnp.bfloat16).astype(jnp.float32)
        meta = jnp.concatenate([number.T, weight.T], axis=0)
        rid = np_rid(w_gate.shape[0], slots)
        xg, c, h = gather_call(slots, x, meta, rid, w_gate, w_up)
        out = jnp.einsum("erf,efd->erd", h, w_down, preferred_element_type=jnp.float32).astype(jnp.bfloat16)
        out = out.reshape(4, CHIPS, 2 * slots, -1).transpose(1, 0, 2, 3).reshape(CHIPS, 8 * slots, -1)
        y = jnp.einsum("pctr,prd->pctd", c, out, preferred_element_type=jnp.float32).astype(jnp.bfloat16)
        y = lax.psum_scatter(y.reshape(16, tokens, -1), "ep", scatter_dimension=0, tiled=False)
        return y[None, None]

    own = P("dp", "ep", None, None)
    return jax.shard_map(
        step, mesh=mesh,
        in_specs=(own, own, own, own, P("ep", None, None), P("ep", None, None), P("ep", None, None)),
        out_specs=own, check_vma=False,
    )
```

time: 773 us -> 621 us (0.80)
  blocking collectives: 236 us -> 0 us
  Pallas kernels: 0 us -> 171 us
  matrix products: 161 us -> 69.6 us
  between operations: 0.11 us -> 13.4 us
  local copies, waits for them, and re-layouts: 31.3 us -> 19.3 us
    reduce_scatter x0 -> x1, waiting for transfers between devices: none -> 341 us  [step(): lax.psum_scatter(y.reshape(16, tokens, -1), 'ep', scatter_dimension=0, ti...]
    another operation x1 -> x0, waiting for transfers between devices: 340 us -> none  [placed(): return lax.with_sharding_constraint(v, NamedSharding(mesh, P(*spec)))]
    another operation x1 -> x0, blocking collectives: 236 us -> none  [placed(): return lax.with_sharding_constraint(v, NamedSharding(mesh, P(*spec)))]
    pallas_call x0 -> x1, Pallas kernels: none -> 171 us  [gather_call(): pl.pallas_call(functools.partial(gather_kernel, slots), out_shape=(jax.Sh...]
    dot_general x7 -> x2, matrix products: 161 us -> 69.6 us  [the longest x1 41.3 us: step(): jnp.einsum('erf,efd->erd', h, w_down, preferred_element_type=jnp.float32)]
    transpose x0 -> x1, local copies, waits for them, and re-layouts: none -> 17.8 us  [step(): out.reshape(4, CHIPS, 2 * slots, -1).transpose(1, 0, 2, 3)]
    another operation x1 -> x0, local copies, waits for them, and re-layouts: 17.5 us -> none  [placed(): return lax.with_sharding_constraint(v, NamedSharding(mesh, P(*spec)))]
    convert_element_type x3 -> x0, local copies, waits for them, and re-layouts: 11.4 us -> none  [the longest x1 5.62 us: step(): einsum('abtke,abtkc->abtec', to_expert, to_slot).astype(jnp.bfloat16)]
  transfers between devices with their start and end apart: 1 -> 1, of which waited for: 1 -> 1; matrix products, arithmetic and copies ran while one was open for 1% -> 0% of each run, Pallas kernels for 0% -> 0%
where the time goes in v1:
time: 621 us; the launch traced here: 617 us
  waiting for transfers between devices  341 us (55%)
  Pallas kernels  171 us (28%)
  matrix products  69.6 us (11%)
  local copies, waits for them, and re-layouts  19.3 us (3%)
  between operations  13.4 us (2%)
    reduce_scatter x1, waiting for transfers between devices, step(): lax.psum_scatter(y.reshape(16, tokens, -1), 'ep', scatter_dimension=0, ti...  341 us
    pallas_call x1, Pallas kernels, gather_call(): pl.pallas_call(functools.partial(gather_kernel, slots), out_shape=(jax.Sh...  171 us
    dot_general x1, matrix products, step(): jnp.einsum('erf,efd->erd', h, w_down, preferred_element_type=jnp.float32)  41.3 us
    dot_general x1, matrix products, step(): jnp.einsum('pctr,prd->pctd', c, out, preferred_element_type=jnp.float32)  28.3 us
    transpose x1, local copies, waits for them, and re-layouts, step(): out.reshape(4, CHIPS, 2 * slots, -1).transpose(1, 0, 2, 3)  17.8 us
  transfers between devices with their start and end apart: 1, of which 1 were waited for; matrix products, arithmetic and copies ran while one was open for 0% of the time, Pallas kernels for 0%

profile of v1, /device:TPU:0, one launch (start us, length us, event | category | flops | bytes accessed | tf_op | source)
XLA Modules:
  0.0 616.7 jit_solution(95414986884971724)
XLA Ops:
  6.5 0.0 reduce-scatter.2.cloned.1.call-start
  6.5 0.7 convert_bitcast_fusion
  7.2 0.7 convert_bitcast_fusion.1
  8.0 0.6 pad_maximum_fusion.meta_ref
  8.6 1.6 broadcast_in_dim.11.rid_ref
  10.1 171.1 %gather_up.1 = (bf16[8,2,256,4096]{3,2,1,0:T(8,128)(2,1)}, bf16[8,2,256,320]{3,2,1,0:T(8,128)(2,1)}, bf16[4,640,1536]{2,1,0:T(8,128)(2,1)}) custom-call(bf16[256,4096]{1,0:T(8,128)(2,1)} %bitcast.27, f32[16,256]{1,0:T(8,128)} %pad_maximum_fusion.meta_ref, f32[2,320,128]{2,1,0:T(8,128)} %broadcast_in_dim.11.rid_ref, bf16[4,4096,1536]{2,1,0:T(8,128)(2,1)} %wg_ref.1, ...), custom_call_target="tpu_custom_call" | custom-call | tf_op jit(solution)/shard_map/gather_up/pallas_call | solution.py:270
  181.2 41.3 %convolution_convert_fusion.1 = bf16[4,640,4096]{2,1,0:T(8,128)(2,1)} fusion(bf16[4,640,1536]{2,1,0:T(8,128)(2,1)} %get-tuple-element.8, bf16[4,1536,4096]{2,1,0:T(8,128)(2,1)} %param.14), kind=kOutput, calls=%fused_computation.1 | convolution fusion | flops 32222740480 | bytes 79167488 | tf_op jit(solution)/shard_map/erf,efd->erd/dot_general | solution.py:318
  222.5 0.0 copy-start
  222.5 17.8 %copy.9 = bf16[8,4,80,4096]{3,2,1,0:T(8,128)(2,1)} copy(bf16[8,4,80,4096]{3,2,0,1:T(8,128)(2,1)} %bitcast.26) | data formatting | bytes 41943040 | tf_op jit(solution)/shard_map/transpose | solution.py:319
  240.3 0.0 copy-done
  240.3 28.3 %convolution_convert_fusion = bf16[8,2,256,4096]{3,2,1,0:T(8,128)(2,1)} fusion(bf16[8,2,256,320]{3,2,1,0:T(8,128)(2,1)S(1)} %copy-done, bf16[8,320,4096,1]{2,1,3,0:T(8,128)(2,1)} %bitcast.25), kind=kOutput, calls=%fused_computation | convolution fusion | flops 10754195456 | bytes 57147392 | tf_op jit(solution)/shard_map/pctr,prd->pctd/dot_general | solution.py:320
  268.6 0.0 reduce-scatter.2.cloned.1.call-update
  268.6 341.2 %reduce-scatter.2.cloned.1.call-done = bf16[1,256,4096]{2,1,0:T(8,128)(2,1)} async-done(((bf16[16,256,4096]{2,1,0:T(8,128)(2,1)}), bf16[1,256,4096]{2,1,0:T(8,128)(2,1)}) %reduce-scatter.2.cloned.1.call-update) | async-done | bytes 2097168 | tf_op jit(solution)/shard_map/reduce_scatter | solution.py:321
Async XLA Ops:
  6.5 603.3 %reduce-scatter.2.cloned.1.call-start = ((), (), s32[]{:S(2)}) async-start(), calls=%async_computation.1 | async-start | bytes 35651584 | tf_op jit(solution)/shard_map/reduce_scatter | solution.py:321
  222.5 17.8 %copy-start = (bf16[8,2,256,320]{3,2,1,0:T(8,128)(2,1)S(1)}, bf16[8,2,256,320]{3,2,1,0:T(8,128)(2,1)}, u32[]{:S(2)}) copy-start(bf16[8,2,256,320]{3,2,1,0:T(8,128)(2,1)} %get-tuple-element.7) | copy-start | bytes 7864324
Sparse Core Ops, SparseCore 0:
  268.8 341.0 reduce-scatter.1
